TPU v7x, 8 devices: a whole 2x2x1 slice. The times are simulated.
8 devices in a mesh: dp: 2 (over z, y), ep: 4 (over x, core).
Axes of the slice: x: 2, y: 2, z: 1, core: 2. Of those that a mesh axis runs over, the one named last changes fastest.
Arguments:
- tok_x: bfloat16 [512, 2048], P(('dp', 'ep')), parts along dimension 0
- route_ids: int32 [512, 8], P(('dp', 'ep')), parts along dimension 0
- route_gate: float32 [512, 8], P(('dp', 'ep')), parts along dimension 0
- w_in: bfloat16 [128, 2048, 768], P('ep')
- w_out: bfloat16 [128, 768, 2048], P('ep')
- shared_in: bfloat16 [2048, 768], replicated
- shared_out: bfloat16 [768, 2048], replicated
Outputs:
- output: bfloat16 [512, 2048], P(('dp', 'ep')), parts along dimension 0
There are 2 independent parts. A program takes and returns all parts, laid end to end along the dimension named above; an argument that names none is the same for every part.
All inputs are finite; a program needn't handle non-finite values.
Results may differ from a plain program's by a relative error of at most 0.00521982.
Values are sent between devices in bfloat16 or wider.
A program may use at most 1 GiB of HBM per device.

v0:
```python
import jax
import jax.numpy as jnp
from jax import lax
from jax.sharding import PartitionSpec as P


def solution(mesh):
    group_size = mesh.shape['ep']

    def device_layer(tok_x, route_ids, route_gate, w_in, w_out, shared_in, shared_out):
        tokens, width = tok_x.shape
        top_k = route_ids.shape[1]
        local_experts = w_in.shape[0]
        experts = local_experts * group_size
        capacity = tokens * group_size * top_k // experts
        local_cap = 2 * tokens * top_k // experts
        flat_ids = route_ids.reshape(-1)
        onehot = (flat_ids[:, None] == jnp.arange(experts, dtype=jnp.int32)[None, :]).astype(jnp.int32)
        running = jnp.cumsum(onehot, axis=0)
        local_rank = jnp.sum(running * onehot, axis=1) - 1
        counts = running[-1]
        pair_pos = flat_ids * local_cap + local_rank
        pair_tok = jnp.arange(tokens * top_k, dtype=jnp.int32) // top_k
        send_tok = jnp.zeros((experts * local_cap,), jnp.int32).at[pair_pos].set(pair_tok)
        send_rows = tok_x[send_tok].reshape(group_size, local_experts, local_cap, width)
        src_counts = lax.all_to_all(counts.reshape(group_size, local_experts), 'ep', 0, 0, tiled=True)
        recv_rows = lax.all_to_all(send_rows, 'ep', 0, 0, tiled=True)
        src_off = jnp.cumsum(src_counts, axis=0) - src_counts
        src_end = src_off + src_counts
        slot_ids = jnp.arange(capacity, dtype=jnp.int32)
        slot_src = jax.vmap(lambda run_end: jnp.searchsorted(run_end, slot_ids, side='right'), in_axes=1)(src_end)
        slot_src = jnp.minimum(slot_src, group_size - 1)
        slot_rank = jnp.clip(slot_ids[None, :] - jnp.take_along_axis(src_off.T, slot_src, axis=1), 0, local_cap - 1)
        expert_col = jnp.arange(local_experts, dtype=jnp.int32)[:, None]
        buffer = recv_rows.reshape(-1, width)[(slot_src * local_experts + expert_col) * local_cap + slot_rank]
        hidden = jax.nn.gelu(jnp.einsum('ecd,edf->ecf', buffer, w_in, preferred_element_type=jnp.float32)).astype(jnp.bfloat16)
        expert_out = jnp.einsum('ecf,efd->ecd', hidden, w_out, preferred_element_type=jnp.float32).astype(jnp.bfloat16)
        ret_slot = src_off[:, :, None] + jnp.arange(local_cap, dtype=jnp.int32)[None, None, :]
        ret_at = expert_col[None, :, :] * capacity + jnp.minimum(ret_slot, capacity - 1)
        back_rows = jnp.where((ret_slot < capacity)[..., None], expert_out.reshape(-1, width)[ret_at], 0)
        home_rows = lax.all_to_all(back_rows, 'ep', 0, 0, tiled=True)
        got_rows = home_rows.reshape(-1, width)[pair_pos].reshape(tokens, top_k, width)
        moe_sum = jnp.sum(route_gate[:, :, None] * got_rows.astype(jnp.float32), axis=1)
        shared_hidden = jax.nn.gelu(jnp.dot(tok_x, shared_in, preferred_element_type=jnp.float32)).astype(jnp.bfloat16)
        shared_y = jnp.dot(shared_hidden, shared_out, preferred_element_type=jnp.float32).astype(jnp.bfloat16)
        return (tok_x.astype(jnp.float32) + shared_y.astype(jnp.float32) + moe_sum).astype(jnp.bfloat16)

    row_spec = P(('dp', 'ep'), None)
    expert_spec = P('ep', None, None)
    whole_spec = P(None, None)
    return jax.shard_map(device_layer, mesh=mesh, in_specs=(row_spec, row_spec, row_spec, expert_spec, expert_spec, whole_spec, whole_spec), out_specs=row_spec, check_vma=False)
```

profile of v0, /device:TPU:0, one launch (start us, length us, event | category | flops | bytes accessed | tf_op | source)
XLA Modules:
  0.0 235.4 jit_solution(3020258182175527198)
XLA Ops:
  0.0 0.9 copy.16
  0.9 0.1 eq.25
  1.0 0.1 copy.17
  1.1 0.2 fusion.20
  1.4 0.0 copy-start.2
  1.4 0.7 copy-done.2
  2.1 1.0 broadcast_add_fusion
  3.1 0.0 copy-start.3
  3.1 0.7 copy-done.3
  3.8 0.7 all_to_all.14
  4.5 4.6 %all-to-all-start = ((s32[4,1,32]{2,1,0:T(1,128)}), s32[4,1,32]{2,1,0:T(1,128)S(1)}, u32[]{:S(2)}, u32[]{:S(2)}) async-start(s32[4,1,32]{2,1,0:T(1,128)} %bitcast.3), calls=%async_computation | async-start | bytes 4096 | tf_op jit(solution)/shard_map/all_to_all | solution.py:26
  9.1 0.1 eq.29
  9.2 0.7 broadcast_multiply_fusion
  9.9 1.2 select_reduce_fusion
  11.1 0.1 copy.20
  11.2 0.1 mul.102
  11.3 2.4 %scatter_custom_fusion = s32[1024]{0:T(1024)S(1)} fusion(s32[512]{0:T(512)S(1)} %bitcast.64, s32[512]{0:T(512)S(1)} %add_select_fusion, s32[]{:T(128)} %constant.93.clone.1), kind=kCustom, calls=%fused_computation.75 | custom fusion | bytes 4100 | tf_op jit(solution)/shard_map/scatter | solution.py:24
  13.8 6.0 %gather_fusion.1 = bf16[1024,2048]{1,0:T(8,128)(2,1)} fusion(bf16[64,2048]{1,0:T(8,128)(2,1)S(1)} %copy-done.1, s32[1024]{0:T(1024)S(1)} %fusion.36), kind=kCustom, calls=%fused_computation.1 | custom fusion | bytes 8392704 | tf_op jit(solution)/shard_map/gather | solution.py:25
  19.8 5.0 %all-to-all-start.1 = ((bf16[4,32,8,2048]{3,2,1,0:T(8,128)(2,1)}), bf16[4,32,8,2048]{3,2,1,0:T(8,128)(2,1)}, u32[]{:S(2)}, u32[]{:S(2)}) async-start(bf16[4,32,8,2048]{3,2,1,0:T(8,128)(2,1)} %bitcast.55), calls=%async_computation.1 | async-start | bytes 8388608 | tf_op jit(solution)/shard_map/all_to_all | solution.py:27
  24.9 14.8 %while.24 = (s32[]{:T(128)}, u32[32,16]{1,0:T(8,128)S(1)}, u32[32,16]{1,0:T(8,128)S(1)}, s32[32,4]{0,1:T(4,128)S(1)}, s32[]{:T(128)}, /*index=5*/s32[]{:T(128)}) while((s32[]{:T(128)}, u32[32,16]{1,0:T(8,128)S(1)}, u32[32,16]{1,0:T(8,128)S(1)}, s32[32,4]{0,1:T(4,128)S(1)}, s32[]{:T(128)}, /*index=5*/s32[]{:T(128)}) %tuple.36), condition=%wide.region_6.7_spmd.clone, body=%wide.region_5.6_spmd.clone.sunk | while | flops 11779 | bytes 42065 | solution.py:31
  24.9 0.1 reshape.209
  25.0 4.7 %gather_fusion = s32[512]{0:T(512)S(1)} fusion(s32[32,4]{0,1:T(4,128)S(1)} %get-tuple-element.142, u32[512]{0:T(512)S(1)} %reshape.209), kind=kCustom, calls=%fused_computation.clone.clone.1 | custom fusion | bytes 8192 | tf_op jit(solution)/shard_map/vmap(jit(searchsorted))/vmap(jit(_searchsorted_scan_impl))/while/body/eval_jaxpr/gather | solution.py:31
  29.7 0.1 squeeze.8
  29.9 0.1 reshape.209
  30.0 4.7 %gather_fusion = s32[512]{0:T(512)S(1)} fusion(s32[32,4]{0,1:T(4,128)S(1)} %get-tuple-element.142, u32[512]{0:T(512)S(1)} %reshape.209), kind=kCustom, calls=%fused_computation.clone.clone.1 | custom fusion | bytes 8192 | tf_op jit(solution)/shard_map/vmap(jit(searchsorted))/vmap(jit(_searchsorted_scan_impl))/while/body/eval_jaxpr/gather | solution.py:31
  34.7 0.1 squeeze.8
  34.8 0.1 reshape.209
  34.9 4.7 %gather_fusion = s32[512]{0:T(512)S(1)} fusion(s32[32,4]{0,1:T(4,128)S(1)} %get-tuple-element.142, u32[512]{0:T(512)S(1)} %reshape.209), kind=kCustom, calls=%fused_computation.clone.clone.1 | custom fusion | bytes 8192 | tf_op jit(solution)/shard_map/vmap(jit(searchsorted))/vmap(jit(_searchsorted_scan_impl))/while/body/eval_jaxpr/gather | solution.py:31
  39.6 0.1 squeeze.8
  39.8 0.1 reshape.161
  39.8 4.7 %gather_fusion.5 = s32[512]{0:T(512)S(1)} fusion(s32[32,4]{0,1:T(4,128)S(1)} %bitcast.53, s32[512]{0:T(512)S(1)} %reshape.161), kind=kCustom, calls=%fused_computation.5 | custom fusion | bytes 8192 | tf_op jit(solution)/shard_map/jit(take_along_axis)/gather | solution.py:33
  44.5 0.1 reshape.164
  44.6 0.1 reshape.139
  44.7 0.1 compare_select_fusion
  44.8 0.1 reshape.147
  44.9 0.1 add_compare_fusion
  45.0 27.7 %all-to-all-done.1 = bf16[4,32,8,2048]{3,2,1,0:T(8,128)(2,1)} async-done(((bf16[4,32,8,2048]{3,2,1,0:T(8,128)(2,1)}), bf16[4,32,8,2048]{3,2,1,0:T(8,128)(2,1)}, u32[]{:S(2)}, u32[]{:S(2)}) %all-to-all-start.1) | async-done | bytes 4194336 | tf_op jit(solution)/shard_map/all_to_all | solution.py:27
  72.7 8.0 %gather_fusion.2 = bf16[512,2048]{1,0:T(8,128)(2,1)} fusion(bf16[1024,2048]{1,0:T(8,128)(2,1)} %bitcast.9, s32[1024]{0:T(1024)S(1)} %pad_clamp_fusion.1), kind=kCustom, calls=%fused_computation.2 | custom fusion | bytes 4196352 | tf_op jit(solution)/shard_map/gather | solution.py:35
  80.7 35.3 %fusion.69 = bf16[32,16,768]{2,1,0:T(8,128)(2,1)} fusion(bf16[32,16,2048]{2,1,0:T(8,128)(2,1)} %bitcast.57, bf16[32,2048,768]{2,1,0:T(8,128)(2,1)} %param.12), kind=kOutput, calls=%fused_computation.30.clone.clone.1 | convolution fusion | flops 1614151680 | bytes 103546880 | tf_op jit(solution)/shard_map/ecd,edf->ecf/dot_general | solution.py:36
  116.1 34.9 %convolution_convert_fusion = bf16[32,16,2048]{2,1,0:T(8,128)(2,1)} fusion(bf16[32,768,2048]{2,1,0:T(8,128)(2,1)} %param.13, bf16[32,16,768]{2,1,0:T(8,128)(2,1)} %fusion.69), kind=kOutput, calls=%fused_computation.16 | convolution fusion | flops 1611661312 | bytes 103546880 | tf_op jit(solution)/shard_map/ecf,efd->ecd/dot_general | solution.py:37
  151.0 10.7 %gather_fusion.3 = bf16[1024,2048]{1,0:T(8,128)(2,1)} fusion(bf16[512,2048]{1,0:T(8,128)(2,1)} %bitcast.54, s32[1024]{0:T(1024)S(1)} %broadcast_clamp_fusion), kind=kCustom, calls=%fused_computation.3 | custom fusion | bytes 8392704 | tf_op jit(solution)/shard_map/gather | solution.py:40
  161.7 4.5 %broadcast_select_fusion = bf16[4,32,8,2048]{3,2,1,0:T(8,128)(2,1)} fusion(bf16[4,32,8,2048]{3,2,1,0:T(8,128)(2,1)} %bitcast.56, pred[4,32,8]{2,1,0:T(8,128)(4,1)S(1)} %add_compare_fusion), kind=kLoop, calls=%fused_computation.15 | loop fusion | flops 2097152 | bytes 8389632 | tf_op jit(solution)/shard_map/jit(_where)/select_n | solution.py:40
  166.2 5.2 %all-to-all-start.2 = ((bf16[4,32,8,2048]{3,2,1,0:T(8,128)(2,1)}), bf16[4,32,8,2048]{3,2,1,0:T(8,128)(2,1)}, u32[]{:S(2)}, u32[]{:S(2)}) async-start(bf16[4,32,8,2048]{3,2,1,0:T(8,128)(2,1)} %broadcast_select_fusion), calls=%async_computation.2 | async-start | bytes 8388608 | tf_op jit(solution)/shard_map/all_to_all | solution.py:41
  171.4 0.1 copy.15
  171.5 47.6 %all-to-all-done.2 = bf16[4,32,8,2048]{3,2,1,0:T(8,128)(2,1)} async-done(((bf16[4,32,8,2048]{3,2,1,0:T(8,128)(2,1)}), bf16[4,32,8,2048]{3,2,1,0:T(8,128)(2,1)}, u32[]{:S(2)}, u32[]{:S(2)}) %all-to-all-start.2) | async-done | bytes 4194336 | tf_op jit(solution)/shard_map/all_to_all | solution.py:41
  219.1 8.0 %gather_fusion.4 = bf16[512,2048]{1,0:T(8,128)(2,1)} fusion(bf16[1024,2048]{1,0:T(8,128)(2,1)} %bitcast.16, s32[1024]{0:T(1024)S(1)} %pad_clamp_fusion), kind=kCustom, calls=%fused_computation.4 | custom fusion | bytes 4196352 | tf_op jit(solution)/shard_map/gather | solution.py:42
  227.1 4.2 %fusion.2 = f32[64,2048]{1,0:T(8,128)} fusion(bf16[512,2048]{1,0:T(8,128)(2,1)} %gather_fusion.4, f32[64,8]{1,0:T(8,128)S(1)} %copy.15), kind=kLoop, calls=%fused_computation.14 | loop fusion | flops 3014656 | bytes 2623488 | tf_op jit(solution)/shard_map/reduce_sum | solution.py:43
  231.3 4.1 %fusion.6 = bf16[64,2048]{1,0:T(8,128)(2,1)} fusion(f32[64,2048]{1,0:T(8,128)} %fusion.2, bf16[768,2048]{1,0:T(8,128)(2,1)S(1)} %copy-done, bf16[64,2048]{1,0:T(8,128)(2,1)S(1)} %copy-done.1, bf16[2048,768]{1,0:T(8,128)(2,1)} %param.14), kind=kOutput, calls=%fused_computation.22 | convolution fusion | flops 403881984 | bytes 7340032 | tf_op jit(solution)/shard_map/dot_general | solution.py:45
  (39 shorter events, 0.3 us)
Async XLA Ops:
  0.0 231.3 %copy-start = (bf16[768,2048]{1,0:T(8,128)(2,1)S(1)}, bf16[768,2048]{1,0:T(8,128)(2,1)}, u32[]{:S(2)}) copy-start(bf16[768,2048]{1,0:T(8,128)(2,1)} %param.15) | copy-start | bytes 9437188
  0.0 13.8 %copy-start.1 = (bf16[64,2048]{1,0:T(8,128)(2,1)S(1)}, bf16[64,2048]{1,0:T(8,128)(2,1)}, u32[]{:S(2)}) copy-start(bf16[64,2048]{1,0:T(8,128)(2,1)} %param.9) | copy-start | bytes 786436
  1.4 0.7 copy-start.2
  3.1 0.7 copy-start.3
  4.5 15.3 %all-to-all-start = ((s32[4,1,32]{2,1,0:T(1,128)}), s32[4,1,32]{2,1,0:T(1,128)S(1)}, u32[]{:S(2)}, u32[]{:S(2)}) async-start(s32[4,1,32]{2,1,0:T(1,128)} %bitcast.3), calls=%async_computation | async-start | bytes 4096 | tf_op jit(solution)/shard_map/all_to_all | solution.py:26
  19.8 52.9 %all-to-all-start.1 = ((bf16[4,32,8,2048]{3,2,1,0:T(8,128)(2,1)}), bf16[4,32,8,2048]{3,2,1,0:T(8,128)(2,1)}, u32[]{:S(2)}, u32[]{:S(2)}) async-start(bf16[4,32,8,2048]{3,2,1,0:T(8,128)(2,1)} %bitcast.55), calls=%async_computation.1 | async-start | bytes 8388608 | tf_op jit(solution)/shard_map/all_to_all | solution.py:27
  166.2 5.2 %copy-start.4 = (f32[64,8]{0,1:T(8,128)S(1)}, f32[64,8]{0,1:T(8,128)}, u32[]{:S(2)}) copy-start(f32[64,8]{0,1:T(8,128)} %param.11) | copy-start | bytes 6148
  166.2 52.9 %all-to-all-start.2 = ((bf16[4,32,8,2048]{3,2,1,0:T(8,128)(2,1)}), bf16[4,32,8,2048]{3,2,1,0:T(8,128)(2,1)}, u32[]{:S(2)}, u32[]{:S(2)}) async-start(bf16[4,32,8,2048]{3,2,1,0:T(8,128)(2,1)} %broadcast_select_fusion), calls=%async_computation.2 | async-start | bytes 8388608 | tf_op jit(solution)/shard_map/all_to_all | solution.py:41
where the time goes:
time: 236 us; the launch traced here: 235 us
  waiting for transfers between devices  75.3 us (32%)
  matrix products  74.3 us (31%)
  local copies, waits for them, and re-layouts  58.3 us (25%)
  starting transfers between devices  14.9 us (6%)
  other arithmetic  12.2 us (5%)
    all_to_all x1, waiting for transfers between devices, device_layer(): home_rows = lax.all_to_all(back_rows, 'ep', 0, 0, tiled=True)  47.6 us
    dot_general x1, matrix products, device_layer(): jnp.einsum('ecd,edf->ecf', buffer, w_in, preferred_element_type=jnp.float32)  35.3 us
    dot_general x1, matrix products, device_layer(): jnp.einsum('ecf,efd->ecd', hidden, w_out, preferred_element_type=jnp.floa...  34.9 us
    all_to_all x1, waiting for transfers between devices, device_layer(): recv_rows = lax.all_to_all(send_rows, 'ep', 0, 0, tiled=True)  27.7 us
    gather x6, local copies, waits for them, and re-layouts, device_layer(): jnp.searchsorted(run_end, slot_ids, side='right')  14.3 us
    gather x1, local copies, waits for them, and re-layouts, device_layer(): expert_out.reshape(-1, width)[ret_at]  10.7 us
    gather x1, local copies, waits for them, and re-layouts, device_layer(): recv_rows.reshape(-1, width)  8 us
    gather x1, local copies, waits for them, and re-layouts, device_layer(): home_rows.reshape(-1, width)[pair_pos].reshape(tokens, top_k, width)  8 us
  transfers between devices with their start and end apart: 3, of which 2 were waited for; matrix products, arithmetic and copies ran while one was open for 13% of the time, Pallas kernels for 0%

commit v1 on v0

v1 whole, which is shorter than its diff:
```python
import functools

import jax
import jax.numpy as jnp
from jax import lax
from jax.experimental import pallas as pl
from jax.experimental.pallas import tpu as pltpu
from jax.sharding import PartitionSpec as P

F32 = jnp.float32
BF16 = jnp.bfloat16
MESH = pl.DeviceIdType.MESH

ROWS = 64
WIDTH = 2048
FF = 768
TOPK = 8
LOCAL = 16
CAP = 16
CK = 256
NCH = WIDTH // CK
EG = 4
KS = 512
NK = WIDTH // KS
NEG = LOCAL // EG
NA = 9
EB = 8
NB = 4
GROUP = 256
META = NCH


def dot(a, b):
    return jnp.dot(a, b, preferred_element_type=F32)


def tdot(a, b):
    return lax.dot_general(a, b, (((0,), (0,)), ((), ())), preferred_element_type=F32)


def bdot(a, b):
    return lax.dot_general(a, b, (((2,), (1,)), ((0,), (0,))), preferred_element_type=F32)


def kernel(x_ref, meta_ref, win_ref, wout_ref, sin_ref, sout_ref, o_ref,
           tok, meta, wa, wb, so, xs, hacc, hid, osc, disp, comb, ypart, r0, r1, r2, hs, ost,
           ld_sem, g1s, g1r, g2s, g2r, gds, gdr, a_sem, b_sem, sh_sem,
           t0s, t0r, t1s, t1r, t2s, t2r, o_sem):
    my_dp = lax.axis_index('dp')
    my_ep = lax.axis_index('ep')
    my_x = my_ep // 2
    my_c = my_ep % 2
    partner = (my_dp, my_x * 2 + (1 - my_c))
    x_nbr = (my_dp, (1 - my_x) * 2 + my_c)
    y_nbr = (1 - my_dp, my_ep)
    e_off = my_dp * LOCAL

    def a_copy(s):
        k, eg = divmod(s, NEG)
        return pltpu.make_async_copy(
            win_ref.at[pl.ds(e_off + eg * EG, EG), pl.ds(k * KS, KS), :], wa.at[s % NA], a_sem.at[s % NA])

    def b_copy(s):
        c, h = divmod(s, LOCAL // EB)
        return pltpu.make_async_copy(
            wout_ref.at[pl.ds(e_off + h * EB, EB), :, pl.ds(c * CK, CK)], wb.at[s % NB], b_sem.at[s % NB])

    def own(i):
        if i == META:
            return meta.at[my_c, my_dp, my_x]
        if i % 2 == 0:
            return tok.at[i, my_c, my_dp, my_x]
        return tok.at[i, my_c, my_x, my_dp]

    def own_pair(i):
        if i == META:
            return meta.at[my_c, my_dp]
        return tok.at[i, my_c, my_dp] if i % 2 == 0 else tok.at[i, my_c, my_x]

    def own_core(i):
        return meta.at[my_c] if i == META else tok.at[i, my_c]

    def load(i):
        src = meta_ref if i == META else x_ref.at[:, pl.ds(i * CK, CK)]
        return pltpu.make_async_copy(src, own(i), ld_sem.at[i])

    def remote(ref, ssem, rsem, i, dev, dst=None):
        return pltpu.make_async_remote_copy(
            src_ref=ref, dst_ref=ref if dst is None else dst, send_sem=ssem.at[i], recv_sem=rsem.at[i],
            device_id=dev, device_id_type=MESH)

    def gather1(i):
        return remote(own(i), g1s, g1r, i, y_nbr if i % 2 and i != META else x_nbr)

    def gather2(i):
        return remote(own_pair(i), g2s, g2r, i, x_nbr if i % 2 and i != META else y_nbr)

    def gatherd(i):
        return remote(own_core(i), gds, gdr, i, partner)

    items = [META] + list(range(NCH))

    for i in items:
        load(i).start()
    for s in range(NA):
        a_copy(s).start()
    for s in range(NB):
        b_copy(s).start()

    barrier = pltpu.get_barrier_semaphore()
    for dev in (partner, x_nbr, y_nbr):
        pl.semaphore_signal(barrier, inc=1, device_id=dev, device_id_type=MESH)
    pl.semaphore_wait(barrier, 3)

    for i in items:
        load(i).wait()
        gather1(i).start()
    for i in items:
        gather1(i).wait_recv()
        gather2(i).start()
    for i in (META, 0, 1):
        gather2(i).wait_recv()
        gatherd(i).start()
    gatherd(META).wait_recv()

    e_id = (lax.broadcasted_iota(jnp.int32, (LOCAL, GROUP), 0) + (my_ep * (2 * LOCAL) + e_off)).astype(F32)
    s_id = lax.broadcasted_iota(jnp.int32, (LOCAL, CAP, GROUP), 1).astype(F32)

    def true_pos(t):
        return ((t // 64) % 2) * 128 + (t // 128) * 64 + t % 64

    before = (true_pos(lax.broadcasted_iota(jnp.int32, (GROUP, GROUP), 0))
              < true_pos(lax.broadcasted_iota(jnp.int32, (GROUP, GROUP), 1)))
    before = jnp.where(before, 1.0, 0.0).astype(BF16)
    eye = (lax.broadcasted_iota(jnp.int32, (GROUP, GROUP), 0)
           == lax.broadcasted_iota(jnp.int32, (GROUP, GROUP), 1))
    eye = jnp.where(eye, 1.0, 0.0).astype(BF16)
    for g in range(2):
        table = jnp.concatenate([meta[0, g, 0] + meta[0, g, 1], meta[1, g, 0] + meta[1, g, 1]], axis=1)
        chosen = jnp.zeros((LOCAL, GROUP), F32)
        gate = jnp.zeros((LOCAL, GROUP), F32)
        for j in range(TOPK):
            hit = table[j:j + 1, :] == e_id
            chosen = jnp.where(hit, 1.0, chosen)
            gate = jnp.where(hit, table[TOPK + j:TOPK + j + 1, :], gate)
        slot = dot(chosen.astype(BF16), before)
        slot = jnp.where(chosen > 0.0, slot, -1.0)
        here = slot[:, None, :] == s_id
        disp[g] = jnp.where(here, 1.0, 0.0).reshape(LOCAL * CAP, GROUP).astype(BF16)
        weight = jnp.where(here, gate[:, None, :], 0.0).reshape(LOCAL * CAP, GROUP)
        for piece in range(3):
            part = weight.astype(BF16)
            comb[g, piece] = tdot(part, eye).astype(BF16)
            weight = weight - part.astype(F32)

    for k in range(NK):
        for h in range(2):
            i = 2 * k + h
            gatherd(i).wait_recv()
            for g in range(2):
                rows = tok[i, :, g] if i % 2 == 0 else tok[i, :, :, g]
                picked = dot(disp[g], rows.reshape(GROUP, CK)).astype(BF16)
                xs[:, pl.ds(g * CAP, CAP), pl.ds(h * CK, CK)] = picked.reshape(LOCAL, CAP, CK)
        for eg in range(NEG):
            s = k * NEG + eg
            a_copy(s).wait()
            batch = pl.ds(eg * EG, EG)
            acc = bdot(xs[batch], wa[s % NA])
            if k > 0:
                acc = acc + hacc[batch]
            if k < NK - 1:
                hacc[batch] = acc
            else:
                hid[batch] = jax.nn.gelu(acc).astype(BF16)
            if s + NA < NK * NEG:
                a_copy(s + NA).start()
            if eg == 1 and k < NK - 1:
                for i in (2 * k + 2, 2 * k + 3):
                    gather2(i).wait_recv()
                    gatherd(i).start()

    def dirs(c):
        if c % 2 == 0:
            return my_x, my_dp, x_nbr, y_nbr
        return my_dp, my_x, y_nbr, x_nbr

    def reduce0(c):
        return remote(ypart.at[c, 1 - my_c], t0s, t0r, c, partner, r0.at[c])

    def reduce1(c):
        a, _, dev, _ = dirs(c)
        return remote(ypart.at[c, my_c, 1 - a], t1s, t1r, c, dev, r1.at[c])

    def reduce2(c):
        a, b, _, dev = dirs(c)
        return remote(ypart.at[c, my_c, a, 1 - b], t2s, t2r, c, dev, r2.at[c])

    def stage1(c):
        a, _, _, _ = dirs(c)
        reduce0(c).wait_recv()
        ypart[c, my_c, 1 - a] = ypart[c, my_c, 1 - a] + r0[c, 1 - a]
        reduce1(c).start()
        ypart[c, my_c, a] = ypart[c, my_c, a] + r0[c, a]

    def stage2(c):
        a, b, _, _ = dirs(c)
        reduce1(c).wait_recv()
        ypart[c, my_c, a, 1 - b] = ypart[c, my_c, a, 1 - b] + r1[c, 1 - b]
        reduce2(c).start()

    def sh_in():
        return pltpu.make_async_copy(sin_ref, wa.at[(NK * NEG) % NA], sh_sem.at[0])

    def sh_out():
        return pltpu.make_async_copy(sout_ref, so, sh_sem.at[1])

    nsteps = NCH * (LOCAL // EB)
    for c in range(NCH):
        for h in range(LOCAL // EB):
            s = c * (LOCAL // EB) + h
            b_copy(s).wait()
            out = bdot(hid[pl.ds(h * EB, EB)], wb[s % NB]).astype(BF16)
            for g in range(2):
                osc[g, pl.ds(h * EB, EB)] = out[:, g * CAP:(g + 1) * CAP]
            if s + NB < nsteps:
                b_copy(s + NB).start()
            elif s + NB == nsteps:
                sh_in().start()
                sh_out().start()
        for g in range(2):
            rows = osc[g].reshape(LOCAL * CAP, CK)
            y = dot(comb[g, 0], rows) + dot(comb[g, 1], rows) + dot(comb[g, 2], rows)
            y = y.reshape(2, 2, ROWS, CK)
            for core in range(2):
                for x in range(2):
                    if c % 2 == 0:
                        ypart[c, core, x, g] = y[core, x]
                    else:
                        ypart[c, core, g, x] = y[core, x]
        reduce0(c).start()
        if c >= 1:
            stage1(c - 1)
        if c >= 3:
            stage2(c - 3)
    stage1(NCH - 1)
    stage2(NCH - 3)

    sh_in().wait()
    acc = jnp.zeros((ROWS, FF), F32)
    for k in range(NK):
        left = own(2 * k)[...]
        right = own(2 * k + 1)[...]
        acc = acc + dot(jnp.concatenate([left, right], axis=1), wa[(NK * NEG) % NA, k])
    hs[...] = jax.nn.gelu(acc).astype(BF16)
    stage2(NCH - 2)
    sh_out().wait()
    stage2(NCH - 1)
    for c in range(NCH):
        shared = dot(hs[...], so[:, pl.ds(c * CK, CK)]).astype(BF16).astype(F32)
        a, b, _, _ = dirs(c)
        reduce2(c).wait_recv()
        moe = ypart[c, my_c, a, b] + r1[c, b] + r2[c]
        ost[:, pl.ds(c * CK, CK)] = (own(c)[...].astype(F32) + shared + moe).astype(BF16)
    out = pltpu.make_async_copy(ost, o_ref, o_sem)
    out.start()
    for i in items:
        gather1(i).wait_send()
        gather2(i).wait_send()
        gatherd(i).wait_send()
    for c in range(NCH):
        reduce0(c).wait_send()
        reduce1(c).wait_send()
        reduce2(c).wait_send()
    out.wait()


def solution(mesh):
    def layer(tok_x, route_ids, route_gate, w_in, w_out, shared_in, shared_out):
        table = jnp.concatenate([route_ids.T.astype(F32), route_gate.T], axis=0)
        first = jnp.pad(table, ((0, 0), (0, 128 - ROWS)))
        second = jnp.pad(table, ((0, 0), (128 - ROWS, 0)))
        table = jnp.where(lax.axis_index('ep') // 2 == 0, first, second)
        hbm = pl.BlockSpec(memory_space=pl.ANY)
        dma = pltpu.SemaphoreType.DMA
        vmem = pltpu.VMEM
        return pl.pallas_call(
            kernel,
            out_shape=jax.ShapeDtypeStruct((ROWS, WIDTH), BF16),
            in_specs=[hbm] * 6,
            out_specs=hbm,
            scratch_shapes=[
                vmem((NCH, 2, 2, 2, ROWS, CK), BF16),
                vmem((2, 2, 2, 2 * TOPK, 128), F32),
                vmem((NA, EG, KS, FF), BF16),
                vmem((NB, EB, FF, CK), BF16),
                vmem((FF, WIDTH), BF16),
                vmem((LOCAL, 2 * CAP, KS), BF16),
                vmem((LOCAL, 2 * CAP, FF), F32),
                vmem((LOCAL, 2 * CAP, FF), BF16),
                vmem((2, LOCAL, CAP, CK), BF16),
                vmem((2, LOCAL * CAP, GROUP), BF16),
                vmem((2, 3, GROUP, LOCAL * CAP), BF16),
                vmem((NCH, 2, 2, 2, ROWS, CK), F32),
                vmem((NCH, 2, 2, ROWS, CK), F32),
                vmem((NCH, 2, ROWS, CK), F32),
                vmem((NCH, ROWS, CK), F32),
                vmem((ROWS, FF), BF16),
                vmem((ROWS, WIDTH), BF16),
                dma((NCH + 1,)),
                dma((NCH + 1,)), dma((NCH + 1,)),
                dma((NCH + 1,)), dma((NCH + 1,)),
                dma((NCH + 1,)), dma((NCH + 1,)),
                dma((NA,)), dma((NB,)), dma((2,)),
                dma((NCH,)), dma((NCH,)), dma((NCH,)), dma((NCH,)), dma((NCH,)), dma((NCH,)),
                dma,
            ],
            compiler_params=pltpu.CompilerParams(
                collective_id=0, has_side_effects=True, vmem_limit_bytes=66_000_000),
            name='moe_layer',
        )(tok_x, table, w_in, w_out, shared_in.reshape(NK, KS, FF), shared_out)

    row_spec = P(('dp', 'ep'), None)
    expert_spec = P('ep', None, None)
    whole_spec = P(None, None)
    return jax.shard_map(layer, mesh=mesh,
                         in_specs=(row_spec, row_spec, row_spec, expert_spec, expert_spec, whole_spec, whole_spec),
                         out_specs=row_spec, check_vma=False)
```

time: 236 us -> 62.8 us (0.27)
  waiting for transfers between devices: 75.3 us -> 0 us
  matrix products: 74.3 us -> 0 us
  Pallas kernels: 0 us -> 58.9 us
  local copies, waits for them, and re-layouts: 58.3 us -> 1.67 us
  starting transfers between devices: 14.9 us -> 0 us
  other arithmetic: 12.2 us -> 2.05 us
    all_to_all x3 -> x0, waiting for transfers between devices: 75.3 us -> none  [the longest x1 47.6 us: device_layer(): home_rows = lax.all_to_all(back_rows, 'ep', 0, 0, tiled=True)]
    dot_general x3 -> x0, matrix products: 74.3 us -> none  [the longest x1 35.3 us: device_layer(): jnp.einsum('ecd,edf->ecf', buffer, w_in, preferred_element_type=jnp.float32)]
    pallas_call x0 -> x1, Pallas kernels: none -> 58.9 us  [layer(): pl.pallas_call(kernel, out_shape=jax.ShapeDtypeStruct((ROWS, WIDTH), BF16...]
    gather x13 -> x0, local copies, waits for them, and re-layouts: 51.9 us -> none  [the longest x6 14.3 us: device_layer(): jnp.searchsorted(run_end, slot_ids, side='right')]
    all_to_all x3 -> x0, starting transfers between devices: 14.9 us -> none  [the longest x1 5.21 us: device_layer(): home_rows = lax.all_to_all(back_rows, 'ep', 0, 0, tiled=True)]
    reduce_sum x2 -> x0, other arithmetic: 5.38 us -> none  [the longest x1 4.2 us: device_layer(): jnp.sum(route_gate[:, :, None] * got_rows.astype(jnp.float32), axis=1)]
    select_n x11 -> x1, other arithmetic: 4.73 us -> 0.68 us  [layer(): table = jnp.where(lax.axis_index('ep') // 2 == 0, first, second)]
    scatter x1 -> x0, local copies, waits for them, and re-layouts: 2.45 us -> none  [device_layer(): jnp.zeros((experts * local_cap,), jnp.int32).at[pair_pos].set(pair_tok)]
  transfers between devices with their start and end apart: 3 -> 0, of which waited for: 2 -> 0; matrix products, arithmetic and copies ran while one was open for 13% -> 0% of each run, Pallas kernels for 0% -> 0%
where the time goes in v1:
time: 62.8 us; the launch traced here: 62.6 us
  Pallas kernels  58.9 us (94%)
  other arithmetic  2.05 us (3%)
  local copies, waits for them, and re-layouts  1.67 us (3%)
    pallas_call x1, Pallas kernels, layer(): pl.pallas_call(kernel, out_shape=jax.ShapeDtypeStruct((ROWS, WIDTH), BF16...  58.9 us
    unnamed x1, local copies, waits for them, and re-layouts  1.67 us

profile of v1, /device:TPU:0, one launch (start us, length us, event | category | flops | bytes accessed | tf_op | source)
XLA Modules:
  0.0 62.6 jit_solution(11811536595882010766)
XLA Ops:
  0.0 0.7 %convert_bitcast_fusion = f32[8,64]{1,0:T(8,128)S(1)} fusion(s32[64,8]{0,1:T(8,128)} %param.8), kind=kLoop, calls=%fused_computation.2 | loop fusion | flops 512 | bytes 4096 | tf_op jit(solution)/shard_map/convert_element_type | solution.py:279
  0.7 0.7 %pad_maximum_fusion = f32[16,64]{1,0:T(8,128)S(1)} fusion(f32[8,64]{1,0:T(8,128)} %bitcast.5, f32[8,64]{1,0:T(8,128)S(1)} %convert_bitcast_fusion), kind=kLoop, calls=%fused_computation | loop fusion | flops 1024 | bytes 8192 | tf_op jit(solution)/shard_map/concatenate | solution.py:279
  1.4 0.7 %pad_select_fusion.meta_ref = f32[16,128]{1,0:T(8,128)} fusion(f32[16,64]{1,0:T(8,128)S(1)} %pad_maximum_fusion, pred[]{:T(512)S(6)} %eq.3), kind=kLoop, calls=%fused_computation.1 | loop fusion | flops 2048 | bytes 12289 | tf_op jit(solution)/shard_map/jit(_where)/select_n | solution.py:282
  2.1 58.9 %moe_layer.1 = bf16[64,2048]{1,0:T(8,128)(2,1)} custom-call(bf16[64,2048]{1,0:T(8,128)(2,1)} %x_ref.1, f32[16,128]{1,0:T(8,128)} %pad_select_fusion.meta_ref, bf16[32,2048,768]{2,1,0:T(8,128)(2,1)} %win_ref.1, bf16[32,768,2048]{2,1,0:T(8,128)(2,1)} %wout_ref.1, bf16[4,512,768]{2,1,0:T(8,128)(2,1)} %bitcast.4, bf16[768,2048]{1,0:T(8,128)(2,1)} %sout_ref.1), custom_call_target="tpu_custom_call" | custom-call | tf_op jit(solution)/shard_map/moe_layer/pallas_call | solution.py:286
  61.0 1.7 %copy.9 = bf16[64,2048]{1,0:T(8,128)(2,1)} copy(bf16[64,2048]{1,0:T(8,128)(2,1)} %moe_layer.1) | data formatting | bytes 524288

commit v2 on v1

v2 whole, which is shorter than its diff:
```python
import jax
import jax.numpy as jnp
from jax import lax
from jax.experimental import pallas as pl
from jax.experimental.pallas import tpu as pltpu
from jax.sharding import PartitionSpec as P

F32 = jnp.float32
BF16 = jnp.bfloat16
MESH = pl.DeviceIdType.MESH

ROWS = 64
WIDTH = 2048
FF = 768
TOPK = 8
LOCAL = 16
CAP = 16
T = 256
NCH = WIDTH // T
EG = 4
KS = 2 * T
NK = WIDTH // KS
NEG = LOCAL // EG
EB = 8
NHB = LOCAL // EB
NF = FF // T
GROUP = 256
NS = 15
A_STEPS = NK * NEG
B_STEPS = NCH * NHB
SH_IN = A_STEPS + B_STEPS
SH_OUT = SH_IN + 1
STEPS = SH_OUT + 1
LAG2 = 4


def dot(a, b):
    return jnp.dot(a, b, preferred_element_type=F32)


def tdot(a, b):
    return lax.dot_general(a, b, (((0,), (0,)), ((), ())), preferred_element_type=F32)


def bdot(a, b):
    return lax.dot_general(a, b, (((2,), (1,)), ((0,), (0,))), preferred_element_type=F32)


def kernel(x_ref, ids_ref, gates_ref, win_ref, wout_ref, sin_ref, sout_ref, o_ref,
           tok, mids, mgates, ring, xs, hacc, hid, osc, disp, comb, ypart, r0, r1, r2, hs, shy, ost,
           ld_sem, g1s, g1r, g2s, g2r, gds, gdr, w_sem, so_sem,
           t0s, t0r, t1s, t1r, t2s, t2r, o_sem):
    my_dp = lax.axis_index('dp')
    my_ep = lax.axis_index('ep')
    my_x = my_ep // 2
    my_c = my_ep % 2
    partner = (my_dp, my_x * 2 + (1 - my_c))
    x_nbr = (my_dp, (1 - my_x) * 2 + my_c)
    y_nbr = (1 - my_dp, my_ep)
    e_off = my_dp * LOCAL

    def w_copies(s):
        slot = s % NS
        if s == SH_OUT:
            return [pltpu.make_async_copy(
                sout_ref.at[:, :, pl.ds(c * T, T)], ring.at[slot, :, c // 2, c % 2], so_sem.at[c]) for c in range(NCH)]
        copies = []
        for n in range(NF):
            if s < A_STEPS:
                k, eg = divmod(s, NEG)
                src = win_ref.at[pl.ds(e_off + eg * EG, EG), pl.ds(2 * k, 2), :, pl.ds(n * T, T)]
            elif s < SH_IN:
                c, h = divmod(s - A_STEPS, NHB)
                src = wout_ref.at[pl.ds(e_off // 2 + h * (EB // 2), EB // 2), :, n, :, pl.ds(c * T, T)]
            else:
                src = sin_ref.at[:, :, :, pl.ds(n * T, T)]
            copies.append(pltpu.make_async_copy(src, ring.at[slot, n], w_sem.at[slot, n]))
        return copies

    def w_start(s):
        if s < STEPS:
            for copy in w_copies(s):
                copy.start()

    def w_wait(s):
        for copy in w_copies(s):
            copy.wait()

    IDS, GATES = NCH, NCH + 1

    def over_y(i):
        return i < NCH and i % 2 == 1

    def buffer(i):
        return mids if i == IDS else mgates if i == GATES else tok.at[i]

    def own_core(i):
        return buffer(i).at[my_c]

    def own_pair(i):
        return buffer(i).at[my_c, my_x if over_y(i) else my_dp]

    def own(i):
        return buffer(i).at[my_c, my_x, my_dp] if over_y(i) else buffer(i).at[my_c, my_dp, my_x]

    def load(i):
        src = ids_ref if i == IDS else gates_ref if i == GATES else x_ref.at[:, pl.ds(i * T, T)]
        return pltpu.make_async_copy(src, own(i), ld_sem.at[i])

    def remote(src, dst, ssem, rsem, dev):
        return pltpu.make_async_remote_copy(
            src_ref=src, dst_ref=dst, send_sem=ssem, recv_sem=rsem, device_id=dev, device_id_type=MESH)

    def gather1(i):
        return remote(own(i), own(i), g1s.at[i], g1r.at[i], y_nbr if over_y(i) else x_nbr)

    def gather2(i):
        return remote(own_pair(i), own_pair(i), g2s.at[i], g2r.at[i], x_nbr if over_y(i) else y_nbr)

    def gatherd(i):
        return remote(own_core(i), own_core(i), gds.at[i], gdr.at[i], partner)

    routing = [IDS, GATES]
    items = routing + list(range(NCH))

    barrier = pltpu.get_barrier_semaphore()
    for dev in (partner, x_nbr, y_nbr):
        pl.semaphore_signal(barrier, inc=1, device_id=dev, device_id_type=MESH)
    for i in items:
        load(i).start()
    for i in items:
        load(i).wait()
    for s in range(NS):
        w_start(s)
    pl.semaphore_wait(barrier, 3)
    for i in items:
        gather1(i).start()
    for i in items:
        gather1(i).wait_recv()
        gather2(i).start()
    for i in routing + [0, 1]:
        gather2(i).wait_recv()
        gatherd(i).start()
    for i in routing:
        gatherd(i).wait_recv()

    e_id = lax.broadcasted_iota(jnp.int32, (LOCAL, GROUP), 0) + (my_ep * (2 * LOCAL) + e_off)
    s_id = lax.broadcasted_iota(jnp.int32, (LOCAL, CAP, GROUP), 1).astype(F32)

    def true_pos(t):
        return ((t // 64) % 2) * 128 + (t // 128) * 64 + t % 64

    t_row = lax.broadcasted_iota(jnp.int32, (GROUP, GROUP), 0)
    t_col = lax.broadcasted_iota(jnp.int32, (GROUP, GROUP), 1)
    before = jnp.where(true_pos(t_row) < true_pos(t_col), 1.0, 0.0).astype(BF16)
    eye = jnp.where(t_row == t_col, 1.0, 0.0).astype(BF16)
    for g in range(2):
        ids = jnp.concatenate([mids[c, g, x] for c in range(2) for x in range(2)], axis=1)
        gates = jnp.concatenate([mgates[c, g, x] for c in range(2) for x in range(2)], axis=1)
        chosen = jnp.zeros((LOCAL, GROUP), F32)
        gate = jnp.zeros((LOCAL, GROUP), F32)
        for j in range(TOPK):
            hit = ids[j:j + 1, :] == e_id
            chosen = jnp.where(hit, 1.0, chosen)
            gate = jnp.where(hit, gates[j:j + 1, :], gate)
        slot = dot(chosen.astype(BF16), before)
        slot = jnp.where(chosen > 0.0, slot, -1.0)
        here = slot[:, None, :] == s_id
        disp[g] = jnp.where(here, 1.0, 0.0).reshape(LOCAL * CAP, GROUP).astype(BF16)
        weight = jnp.where(here, gate[:, None, :], 0.0).reshape(LOCAL * CAP, GROUP)
        for piece in range(3):
            part = weight.astype(BF16)
            comb[g, piece] = tdot(part, eye).astype(BF16)
            weight = weight - part.astype(F32)

    for k in range(NK):
        for h in range(2):
            gatherd(2 * k + h).wait_recv()
        for h in range(2):
            i = 2 * k + h
            for g in range(2):
                rows = tok[i, :, :, g] if over_y(i) else tok[i, :, g]
                picked = dot(disp[g], rows.reshape(GROUP, T)).astype(BF16)
                xs[:, pl.ds(g * CAP, CAP), pl.ds(h * T, T)] = picked.reshape(LOCAL, CAP, T)
        for eg in range(NEG):
            s = k * NEG + eg
            batch = pl.ds(eg * EG, EG)
            w_wait(s)
            for n in range(NF):
                cols = pl.ds(n * T, T)
                acc = bdot(xs[batch], ring[s % NS, n].reshape(EG, KS, T))
                if k > 0:
                    acc = acc + hacc[batch, :, cols]
                if k < NK - 1:
                    hacc[batch, :, cols] = acc
                else:
                    hid[batch, :, cols] = jax.nn.gelu(acc).astype(BF16)
            w_start(s + NS)
            if eg == 1 and k < NK - 1:
                for i in (2 * k + 2, 2 * k + 3):
                    gather2(i).wait_recv()
                    gatherd(i).start()

    def dirs(c):
        if c % 2 == 0:
            return my_x, my_dp, x_nbr, y_nbr
        return my_dp, my_x, y_nbr, x_nbr

    def reduce0(c):
        return remote(ypart.at[c, 1 - my_c], r0.at[c], t0s.at[c], t0r.at[c], partner)

    def reduce1(c, last):
        a, b, dev, _ = dirs(c)
        side = b if last else 1 - b
        return remote(ypart.at[c, my_c, 1 - a, side], r1.at[c, side], t1s.at[c, last], t1r.at[c, last], dev)

    def reduce2(c):
        a, b, _, dev = dirs(c)
        return remote(ypart.at[c, my_c, a, 1 - b], r2.at[c], t2s.at[c], t2r.at[c], dev)

    def stage1(c):
        a, b, _, _ = dirs(c)
        reduce0(c).wait_recv()
        ypart[c, my_c, 1 - a] = ypart[c, my_c, 1 - a] + r0[c, 1 - a]
        reduce1(c, 0).start()
        reduce1(c, 1).start()
        ypart[c, my_c, a] = ypart[c, my_c, a] + r0[c, a]

    def stage2(c):
        a, b, _, _ = dirs(c)
        reduce1(c, 0).wait_recv()
        ypart[c, my_c, a, 1 - b] = ypart[c, my_c, a, 1 - b] + r1[c, 1 - b]
        reduce2(c).start()

    def write(c):
        return pltpu.make_async_copy(ost.at[c], o_ref.at[:, pl.ds(c * T, T)], o_sem.at[c])

    def final(c):
        a, b, _, _ = dirs(c)
        reduce1(c, 1).wait_recv()
        reduce2(c).wait_recv()
        moe = ypart[c, my_c, a, b] + r1[c, b] + r2[c]
        ost[c] = (own(c)[...].astype(F32) + shy[:, pl.ds(c * T, T)].astype(F32) + moe).astype(BF16)
        write(c).start()

    for c in range(NCH):
        for h in range(NHB):
            s = A_STEPS + c * NHB + h
            batch = pl.ds(h * EB, EB)
            w_wait(s)
            out = bdot(hid[batch, :, pl.ds(0, T)], ring[s % NS, 0].reshape(EB, T, T))
            for j in range(1, NF):
                out = out + bdot(hid[batch, :, pl.ds(j * T, T)], ring[s % NS, j].reshape(EB, T, T))
            out = out.astype(BF16)
            for g in range(2):
                osc[g, batch] = out[:, g * CAP:(g + 1) * CAP]
            w_start(s + NS)
        for g in range(2):
            rows = osc[g].reshape(LOCAL * CAP, T)
            y = dot(comb[g, 0], rows) + dot(comb[g, 1], rows) + dot(comb[g, 2], rows)
            y = y.reshape(2, 2, ROWS, T)
            for core in range(2):
                for x in range(2):
                    if c % 2 == 0:
                        ypart[c, core, x, g] = y[core, x]
                    else:
                        ypart[c, core, g, x] = y[core, x]
        reduce0(c).start()
        if c >= 1:
            stage1(c - 1)
        if c >= LAG2:
            stage2(c - LAG2)
    stage1(NCH - 1)

    stage2(NCH - LAG2)
    w_wait(SH_IN)
    for n in range(NF):
        acc = jnp.zeros((ROWS, T), F32)
        weights = ring[SH_IN % NS, n].reshape(NCH, T, T)
        for k in range(NCH):
            acc = acc + dot(own(k)[...], weights[k])
        hs[:, pl.ds(n * T, T)] = jax.nn.gelu(acc).astype(BF16)
    stage2(NCH - LAG2 + 1)
    w_wait(SH_OUT)
    for c in range(NCH):
        acc = jnp.zeros((ROWS, T), F32)
        for j in range(NF):
            acc = acc + dot(hs[:, pl.ds(j * T, T)], ring[SH_OUT % NS, j, c // 2, c % 2])
        shy[:, pl.ds(c * T, T)] = acc.astype(BF16)
    stage2(NCH - 2)
    stage2(NCH - 1)
    for c in range(NCH):
        final(c)
    for i in items:
        gather1(i).wait_send()
        gather2(i).wait_send()
        gatherd(i).wait_send()
    for c in range(NCH):
        reduce0(c).wait_send()
        reduce1(c, 0).wait_send()
        reduce1(c, 1).wait_send()
        reduce2(c).wait_send()
        write(c).wait()


def solution(mesh):
    def layer(tok_x, route_ids, route_gate, w_in, w_out, shared_in, shared_out):
        local = w_in.shape[0]
        any_space = pl.BlockSpec(memory_space=pl.ANY)
        dma = pltpu.SemaphoreType.DMA
        vmem = pltpu.VMEM
        return pl.pallas_call(
            kernel,
            out_shape=jax.ShapeDtypeStruct((ROWS, WIDTH), BF16),
            in_specs=[any_space] * 7,
            out_specs=any_space,
            scratch_shapes=[
                vmem((NCH, 2, 2, 2, ROWS, T), BF16),
                vmem((2, 2, 2, TOPK, ROWS), jnp.int32),
                vmem((2, 2, 2, TOPK, ROWS), F32),
                vmem((NS, NF, EG, 2, T, T), BF16),
                vmem((LOCAL, 2 * CAP, KS), BF16),
                vmem((LOCAL, 2 * CAP, FF), F32),
                vmem((LOCAL, 2 * CAP, FF), BF16),
                vmem((2, LOCAL, CAP, T), BF16),
                vmem((2, LOCAL * CAP, GROUP), BF16),
                vmem((2, 3, GROUP, LOCAL * CAP), BF16),
                vmem((NCH, 2, 2, 2, ROWS, T), F32),
                vmem((NCH, 2, 2, ROWS, T), F32),
                vmem((NCH, 2, ROWS, T), F32),
                vmem((NCH, ROWS, T), F32),
                vmem((ROWS, FF), BF16),
                vmem((ROWS, WIDTH), BF16),
                vmem((NCH, ROWS, T), BF16),
                dma((NCH + 2,)),
                dma((NCH + 2,)), dma((NCH + 2,)),
                dma((NCH + 2,)), dma((NCH + 2,)),
                dma((NCH + 2,)), dma((NCH + 2,)),
                dma((NS, NF)), dma((NCH,)),
                dma((NCH,)), dma((NCH,)), dma((NCH, 2)), dma((NCH, 2)), dma((NCH,)), dma((NCH,)),
                dma((NCH,)),
            ],
            compiler_params=pltpu.CompilerParams(
                collective_id=0, has_side_effects=True, vmem_limit_bytes=67_000_000),
            name='moe_layer',
        )(tok_x, route_ids.T, route_gate.T,
          w_in.reshape(local, WIDTH // T, T, FF), w_out.reshape(local // 2, 2, NF, T, WIDTH),
          shared_in.reshape(EG, 2, T, FF), shared_out.reshape(NF, T, WIDTH))

    row_spec = P(('dp', 'ep'), None)
    expert_spec = P('ep', None, None)
    whole_spec = P(None, None)
    return jax.shard_map(layer, mesh=mesh,
                         in_specs=(row_spec, row_spec, row_spec, expert_spec, expert_spec, whole_spec, whole_spec),
                         out_specs=row_spec, check_vma=False)
```

time: 62.8 us -> 55.4 us (0.88)
  Pallas kernels: 58.9 us -> 53.5 us
  other arithmetic: 2.05 us -> 0 us
    pallas_call x1, Pallas kernels: 58.9 us -> 53.5 us  [layer(): pl.pallas_call(kernel, out_shape=jax.ShapeDtypeStruct((ROWS, WIDTH), BF16...]
    concatenate x1 -> x0, other arithmetic: 0.69 us -> none  [layer(): table = jnp.concatenate([route_ids.T.astype(F32), route_gate.T], axis=0)]
    convert_element_type x1 -> x0, other arithmetic: 0.69 us -> none  [layer(): table = jnp.concatenate([route_ids.T.astype(F32), route_gate.T], axis=0)]
    select_n x1 -> x0, other arithmetic: 0.68 us -> none  [layer(): table = jnp.where(lax.axis_index('ep') // 2 == 0, first, second)]
where the time goes in v2:
time: 55.4 us; the launch traced here: 55.2 us
  Pallas kernels  53.5 us (97%)
  local copies, waits for them, and re-layouts  1.67 us (3%)
    pallas_call x1, Pallas kernels, layer(): pl.pallas_call(kernel, out_shape=jax.ShapeDtypeStruct((ROWS, WIDTH), BF16...  53.5 us
    unnamed x1, local copies, waits for them, and re-layouts  1.67 us

profile of v2, /device:TPU:0, one launch (start us, length us, event | category | flops | bytes accessed | tf_op | source)
XLA Modules:
  0.0 55.2 jit_solution(1466663579561461161)
XLA Ops:
  0.0 53.5 %moe_layer.1 = bf16[64,2048]{1,0:T(8,128)(2,1)} custom-call(bf16[64,2048]{1,0:T(8,128)(2,1)} %x_ref.1, s32[8,64]{1,0:T(8,128)} %bitcast.8, f32[8,64]{1,0:T(8,128)} %bitcast.9, bf16[32,8,256,768]{3,2,1,0:T(8,128)(2,1)} %bitcast.2.win_ref, bf16[16,2,3,256,2048]{4,3,2,1,0:T(8,128)(2,1)} %bitcast.3.wout_ref, bf16[4,2,256,768]{3,2,1,0:T(8,128)(2,1)} %bitcast.6, ...), custom_call_target="tpu_custom_call" | custom-call | tf_op jit(solution)/shard_map/moe_layer/pallas_call | solution.py:312
  53.5 1.7 %copy.9 = bf16[64,2048]{1,0:T(8,128)(2,1)} copy(bf16[64,2048]{1,0:T(8,128)(2,1)} %moe_layer.1) | data formatting | bytes 524288
